TPU v7x, 32 devices: a whole 2x2x4 slice. The times are simulated.
32 devices in a mesh: seq: 4 (over y, core), tp: 8 (over z, x).
Axes of the slice: x: 2, y: 2, z: 4, core: 2. Of those that a mesh axis runs over, the one named last changes fastest.
Arguments:
- tokens: bfloat16 [4096, 5376], P('seq'), may hold values from -6 to 6
- pre_gain: float32 [5376], replicated, may hold values from 0.5 to 2
- w_query: bfloat16 [5376, 4096], P(None, 'tp'), may hold values from -0.078125 to 0.078125
- key_weight_matrix: bfloat16 [5376, 2048], P(None, 'tp'), may hold values from -0.078125 to 0.078125
- value_weight_matrix: bfloat16 [5376, 2048], P(None, 'tp'), may hold values from -0.078125 to 0.078125
- query_gain: float32 [128], replicated, may hold values from 0.5 to 9
- key_norm_gain: float32 [128], replicated, may hold values from 0.5 to 9
- prior_key_cache: bfloat16 [1024, 2048], P(None, 'tp'), may hold values from -6 to 6
- prior_value_cache: bfloat16 [1024, 2048], P(None, 'tp'), may hold values from -6 to 6
- w_out: bfloat16 [4096, 5376], P('tp'), may hold values from -0.09375 to 0.09375
- post_gain: float32 [5376], replicated, may hold values from 0.5 to 2
Outputs:
- updated: bfloat16 [4096, 5376], P(('seq', 'tp'))
All inputs are finite; a program needn't handle non-finite values.
Results may differ from a plain program's by a relative error of at most 0.015.
The roundings to bfloat16 on the way count: a program that leaves them out, or rounds other values in their place, can miss the bound.
Values may be sent and summed in bfloat16 or wider, within the bound.
A program may use at most 128 MiB of HBM per device.

v0:
```python
import functools

import jax
import jax.numpy as jnp
from jax import lax
from jax.experimental import pallas as pl
from jax.experimental.pallas import tpu as pltpu
from jax.sharding import PartitionSpec as P

MODEL_WIDTH = 5376
HQ = 32
WINDOW_SPAN = 1024
EPSILON = 1e-06
LANES = 128
MESH = pl.DeviceIdType.MESH


def rotary_tables(half, token_positions):
    exponent = jnp.arange(half, dtype=jnp.float32) * (-1.0 / half)
    frequency = jnp.power(jnp.float32(10000.0), exponent)
    angles = token_positions.astype(jnp.float32)[:, None] * frequency[None, :]
    return jnp.cos(angles), jnp.sin(angles)


def chunk_count(width):
    for unit in (256, 128):
        if width % unit == 0:
            tiles = width // unit
            return max(n for n in range(1, 8) if tiles % n == 0)
    return 1


def orders(places):
    return [
        sorted(range(places), key=lambda r: (-abs(r - p), r < p)) for p in range(places)
    ]


def flipped(index, bit):
    return index + bit - 2 * bit * ((index // bit) % 2)


def kernel(
    dims,
    tokens_ref, wq_ref, wk_ref, wv_ref, pk_ref, pv_ref, wo_ref,
    pre_ref, post_ref, qg_ref, kg_ref, cos_ref, sin_ref,
    out_ref,
    x_buf, wq_buf, wk_buf, wv_buf, q_buf, k_buf, v_buf, wo_buf, wx_buf, att_buf, got_buf, slots, acc_buf, own_buf,
    tok_sem, w_sem, prior_sem, wo_sem, own_sem, w_send, w_recv, kv_send, kv_recv, sw_send, sw_recv, s_send, s_recv,
):
    seq, tp, head, chunks = dims
    rows, width = tokens_ref.shape
    places = tp // 2
    local = rows // tp
    count = 2 * local
    w_rows = wo_ref.shape[0]
    piece = w_rows // seq
    cols = width // chunks
    bits = []
    bit = seq // 2
    while bit >= 1:
        bits.append(bit)
        bit //= 2
    stages = len(bits)
    s = lax.axis_index("seq")
    t = lax.axis_index("tp")
    side = t % 2
    p = t // 2
    mate = t + 1 - 2 * side
    scale = float(MODEL_WIDTH // HQ) ** (-0.5)
    f32 = jnp.float32

    parts = 4
    part = rows // parts

    def token_load(i):
        return pltpu.make_async_copy(tokens_ref.at[pl.ds(i * part, part)], x_buf.at[pl.ds(i * part, part)], tok_sem.at[i])

    def wo_load(c):
        return pltpu.make_async_copy(wo_ref.at[:, pl.ds(c * cols, cols)], wo_buf.at[c], wo_sem.at[c])

    weight_loads = [
        pltpu.make_async_copy(src, dst, w_sem.at[i])
        for i, (src, dst) in enumerate(((wk_ref, wk_buf), (wv_ref, wv_buf), (wq_ref, wq_buf)))
    ]
    prior_loads = [
        pltpu.make_async_copy(src, dst.at[pl.ds(0, WINDOW_SPAN)], prior_sem.at[i])
        for i, (src, dst) in enumerate(((pk_ref, k_buf), (pv_ref, v_buf)))
    ]
    own_load = pltpu.make_async_copy(tokens_ref.at[pl.ds(pl.multiple_of(t * local, local), local)], own_buf, own_sem)
    for i in range(parts):
        token_load(i).start()
    for load in weight_loads:
        load.start()

    @pl.when(s == 0)
    def _():
        for load in prior_loads:
            load.start()

    barrier = pltpu.get_barrier_semaphore()
    near = [(None, (s, mate))]
    near += [(None, (flipped(s, b), t)) for b in bits]
    near += [((s > 0) & (s % 2 == 0), (s - 1, t)), ((s < seq - 1) & (s % 2 == 1), (s + 1, t))]
    near += [(p > 0, (s, t - 2)), (p < places - 1, (s, t + 2))]
    peers = 0
    for there, device in near:
        if there is None:
            peers = peers + 1
            pl.semaphore_signal(barrier, inc=1, device_id=device, device_id_type=MESH)
        else:
            peers = peers + jnp.where(there, 1, 0)

            @pl.when(there)
            def _(device=device):
                pl.semaphore_signal(barrier, inc=1, device_id=device, device_id_type=MESH)
    pl.semaphore_wait(barrier, peers)

    def w_piece(c, index):
        return wx_buf.at[c, pl.ds(pl.multiple_of(index * piece, piece), piece)]

    def w_first(c):
        return pltpu.make_async_remote_copy(
            src_ref=wo_ref.at[pl.ds(pl.multiple_of(s * piece, piece), piece), pl.ds(c * cols, cols)],
            dst_ref=w_piece(c, s),
            send_sem=w_send.at[c, 0],
            recv_sem=w_recv.at[c, 0],
            device_id=(s, mate),
            device_id_type=MESH,
        )

    def masks(stage):
        held = [0]
        for b in bits[: stage - 1]:
            held = held + [m + b for m in held]
        return held

    def from_mask(m):
        index = s
        for b in bits:
            if m & b:
                index = flipped(index, b)
        return index

    def w_next(c, stage, m):
        b = bits[stage - 1]
        index = from_mask(m)
        return pltpu.make_async_remote_copy(
            src_ref=w_piece(c, index),
            dst_ref=w_piece(c, index),
            send_sem=w_send.at[c, m + b],
            recv_sem=w_recv.at[c, m + b],
            device_id=(flipped(s, b), t),
            device_id_type=MESH,
        )

    def w_arrived(c, m):
        pltpu.make_async_remote_copy(
            src_ref=w_piece(c, from_mask(m)),
            dst_ref=w_piece(c, from_mask(m)),
            send_sem=w_send.at[c, m],
            recv_sem=w_recv.at[c, m],
            device_id=(s, mate),
            device_id_type=MESH,
        ).wait_recv()

    def pump(stage, c):
        if stage == 1:
            w_arrived(c, 0)
        else:
            b = bits[stage - 2]
            for m in masks(stage - 1):
                w_arrived(c, m + b)
        for m in masks(stage):
            w_next(c, stage, m).start()

    def pumps(position):
        for stage in range(1, stages + 1):
            lag = -1 if stage == 1 else stage - 1
            if isinstance(position, int):
                if position == 0 and stage == 1:
                    pump(1, 0)
                c = position - lag
                if 0 <= c < chunks:
                    pump(stage, c)
            else:
                c = position - lag

                @pl.when((c >= 0) & (c < chunks))
                def _(stage=stage, c=c):
                    pump(stage, c)

    def w_ready(c):
        if stages == 0:
            w_arrived(c, 0)
        else:
            b = bits[-1]
            for m in masks(stages):
                w_arrived(c, m + b)
        wo_load(c).wait()

    for c in range(chunks):
        w_first(c).start()
    for c in range(chunks):
        wo_load(c).start()
    own_load.start()

    group = 32
    tiles = width // LANES

    for i in range(parts):
        token_load(i).wait()

        @pl.loop(0, part // group)
        def _(g, i=i):
            at = pl.ds(pl.multiple_of(i * part + g * group, group), group)
            sums = jnp.zeros((group, LANES), f32)
            for j in range(tiles):
                v = x_buf[at, j * LANES : (j + 1) * LANES].astype(f32)
                sums = sums + v * v
            factor = lax.rsqrt(jnp.sum(sums, axis=-1, keepdims=True) * (1.0 / width) + EPSILON)
            for j in range(tiles):
                v = x_buf[at, j * LANES : (j + 1) * LANES].astype(f32)
                gain = pre_ref[:, j * LANES : (j + 1) * LANES]
                x_buf[at, j * LANES : (j + 1) * LANES] = (v * factor * gain).astype(jnp.bfloat16)

    pumps(0)

    row_tile = min(512, rows)

    def project(w_buf, first, size, dst, dst_row, gain_ref):
        @pl.loop(0, rows // row_tile)
        def _(i):
            at = pl.ds(pl.multiple_of(i * row_tile, row_tile), row_tile)
            to = pl.ds(pl.multiple_of(dst_row + i * row_tile, row_tile), row_tile)
            raw = jnp.dot(x_buf[at, :], w_buf[:, first : first + size], preferred_element_type=f32)
            if gain_ref is None:
                dst[to, first : first + size] = raw.astype(jnp.bfloat16)
                return
            cosine = cos_ref[at, :]
            sine = sin_ref[at, :]
            for h in range(size // head):
                u = raw[:, h * head : (h + 1) * head]
                mean_square = jnp.mean(u * u, axis=-1, keepdims=True)
                u = u * lax.rsqrt(mean_square + EPSILON) * gain_ref[...]
                u = u * cosine + pltpu.roll(u, head // 2, 1) * sine
                dst[to, first + h * head : first + (h + 1) * head] = u.astype(jnp.bfloat16)

    def kv_copy(i):
        buf = (k_buf, v_buf)[i]
        return pltpu.make_async_remote_copy(
            src_ref=buf.at[pl.ds(rows, WINDOW_SPAN)],
            dst_ref=buf.at[pl.ds(0, WINDOW_SPAN)],
            send_sem=kv_send.at[i],
            recv_sem=kv_recv.at[i],
            device_id=(s + 1, t),
            device_id_type=MESH,
        )

    q_cols = wq_ref.shape[1]
    kv_cols = wk_ref.shape[1]
    weight_loads[0].wait()
    project(wk_buf, 0, kv_cols, k_buf, WINDOW_SPAN, kg_ref)

    @pl.when(s < seq - 1)
    def _():
        kv_copy(0).start()

    pumps(1)
    weight_loads[1].wait()
    project(wv_buf, 0, kv_cols, v_buf, WINDOW_SPAN, None)

    @pl.when(s < seq - 1)
    def _():
        kv_copy(1).start()

    pumps(2)
    weight_loads[2].wait()
    tile = min(256, q_cols)
    position = 3
    for j in range(q_cols // tile):
        project(wq_buf, j * tile, tile, q_buf, 0, qg_ref)
        pumps(position)
        position += 1

    @pl.when(s == 0)
    def _():
        for load in prior_loads:
            load.wait()

    @pl.when(s > 0)
    def _():
        for i in range(2):
            kv_copy(i).wait_recv()

    table = orders(places)

    def row_block(k):
        r = 0
        for at in range(places):
            for kk in range(places):
                r = r + jnp.where((p == at) & (k == kk), table[at][kk], 0)
        return r

    span = count + WINDOW_SPAN
    group_heads = q_cols // kv_cols

    def attend(k):
        r = row_block(k)
        first = pl.multiple_of(r * count, count)
        row_ids = lax.broadcasted_iota(jnp.int32, (count, span), 0)
        col_ids = lax.broadcasted_iota(jnp.int32, (count, span), 1)
        allowed = (col_ids > row_ids) & (col_ids <= row_ids + WINDOW_SPAN)
        for kv in range(kv_cols // head):
            keys = k_buf[pl.ds(first, span), kv * head : (kv + 1) * head]
            values = v_buf[pl.ds(first, span), kv * head : (kv + 1) * head]
            for g in range(group_heads):
                at = slice((kv * group_heads + g) * head, (kv * group_heads + g + 1) * head)
                scores = lax.dot_general(
                    q_buf[pl.ds(first, count), at], keys, (((1,), (1,)), ((), ())), preferred_element_type=f32
                )
                scores = jnp.where(allowed, scores * scale, -jnp.inf)
                highest = jnp.max(scores, axis=-1, keepdims=True)
                weights = jnp.exp(scores - highest)
                total = jnp.sum(weights, axis=-1, keepdims=True)
                mixed = jnp.dot(weights.astype(jnp.bfloat16), values, preferred_element_type=f32)
                mixed = (mixed / total).astype(jnp.bfloat16)
                att_buf[k, 0, :, at] = mixed[:local]
                att_buf[k, 1, :, at] = mixed[local:]

    def swap(k):
        return pltpu.make_async_remote_copy(
            src_ref=att_buf.at[k, 1 - side],
            dst_ref=got_buf.at[k],
            send_sem=sw_send.at[k],
            recv_sem=sw_recv.at[k],
            device_id=(s, mate),
            device_id_type=MESH,
        )

    def product(k, c):
        return jnp.dot(att_buf[k, side], wo_buf[c], preferred_element_type=f32) + jnp.dot(
            got_buf[k], wx_buf[c], preferred_element_type=f32
        )

    def sum_copy(r, slot, c, place):
        return pltpu.make_async_remote_copy(
            src_ref=slots.at[r, c],
            dst_ref=slots.at[slot, c],
            send_sem=s_send.at[r, c],
            recv_sem=s_recv.at[slot, c],
            device_id=(s, 2 * place + side),
            device_id_type=MESH,
        )

    def push(k, c):
        r = row_block(k)
        right = r > p
        inner = jnp.where(right, p, places - 1 - p) > 0
        total = product(k, c)

        @pl.when(inner)
        def _():
            sum_copy(r, r, c, p).wait_recv()

        total = total + jnp.where(inner, slots[r, c].astype(f32), 0.0)
        slots[r, c] = total.astype(jnp.bfloat16)

        @pl.when(right)
        def _():
            sum_copy(r, r, c, p + 1).start()

        @pl.when(jnp.logical_not(right))
        def _():
            sum_copy(r, jnp.where(r == p - 1, places, r), c, p - 1).start()

    early = min(3, chunks)
    base = position

    @pl.loop(0, places)
    def _(k):
        attend(k)
        swap(k).start()
        pumps(base + k)

        @pl.when(k == 1)
        def _():
            for c in range(early):
                w_ready(c)

        @pl.when(k >= 1)
        def _():
            swap(k - 1).wait_recv()

            @pl.loop(0, early)
            def _(c):
                push(k - 1, c)

    for extra in range(base + places, chunks + stages):
        pumps(extra)

    @pl.loop(early, chunks)
    def _(c):
        w_ready(c)

        @pl.loop(0, places - 1)
        def _(k):
            push(k, c)

    if places == 1:
        for c in range(early):
            w_ready(c)
    last = places - 1
    swap(last).wait_recv()
    own_load.wait()

    def finish(c, square):
        total = product(last, c)

        @pl.when(p > 0)
        def _():
            sum_copy(p, p, c, p).wait_recv()

        @pl.when(p < places - 1)
        def _():
            sum_copy(p, places, c, p).wait_recv()

        total = total + jnp.where(p > 0, slots[p, c].astype(f32), 0.0)
        total = total + jnp.where(p < places - 1, slots[places, c].astype(f32), 0.0)
        acc_buf[c] = total
        return square + jnp.sum(total * total, axis=-1, keepdims=True)

    square = lax.fori_loop(0, chunks, finish, jnp.zeros((local, 1), f32))
    factor = lax.rsqrt(square * (1.0 / width) + EPSILON)
    for c in range(chunks):
        at = slice(c * cols, (c + 1) * cols)
        out_ref[:, at] = (own_buf[:, at].astype(f32) + acc_buf[c] * factor * post_ref[:, at]).astype(out_ref.dtype)

    for c in range(chunks):
        w_first(c).wait_send()
    if stages:
        @pl.loop(0, chunks)
        def _(c):
            for stage in range(1, stages + 1):
                for m in masks(stage):
                    w_next(c, stage, m).wait_send()

    @pl.when(s < seq - 1)
    def _():
        for i in range(2):
            kv_copy(i).wait_send()

    @pl.loop(0, places)
    def _(k):
        swap(k).wait_send()

        @pl.when(k < places - 1)
        def _():
            r = row_block(k)

            @pl.loop(0, chunks)
            def _(c):
                sum_copy(r, r, c, p).wait_send()


def sublayer(
    sizes,
    tokens,
    pre_gain,
    w_query,
    key_weight_matrix,
    value_weight_matrix,
    query_gain,
    key_norm_gain,
    prior_key_cache,
    prior_value_cache,
    w_out,
    post_gain,
):
    seq, tp = sizes
    rows, width = tokens.shape
    head = query_gain.shape[0]
    q_cols, kv_cols = w_query.shape[1], key_weight_matrix.shape[1]
    w_rows = w_out.shape[0]
    local = rows // tp
    places = tp // 2
    chunks = chunk_count(width)
    cols = width // chunks
    token_positions = WINDOW_SPAN + lax.axis_index("seq") * rows + jnp.arange(rows, dtype=jnp.int32)
    cosine, sine = rotary_tables(head // 2, token_positions)
    cosine = jnp.concatenate([cosine, cosine], axis=1)
    sine = jnp.concatenate([-sine, sine], axis=1)
    bf16, f32 = jnp.bfloat16, jnp.float32
    dma = pltpu.SemaphoreType.DMA
    anywhere = pl.BlockSpec(memory_space=pl.ANY)
    vmem = pl.BlockSpec(memory_space=pltpu.VMEM)
    return pl.pallas_call(
        functools.partial(kernel, (seq, tp, head, chunks)),
        out_shape=jax.ShapeDtypeStruct((local, width), tokens.dtype),
        in_specs=[anywhere] * 7 + [vmem] * 6,
        out_specs=vmem,
        scratch_shapes=[
            pltpu.VMEM((rows, width), bf16),
            pltpu.VMEM((width, q_cols), bf16),
            pltpu.VMEM((width, kv_cols), bf16),
            pltpu.VMEM((width, kv_cols), bf16),
            pltpu.VMEM((rows, q_cols), bf16),
            pltpu.VMEM((WINDOW_SPAN + rows, kv_cols), bf16),
            pltpu.VMEM((WINDOW_SPAN + rows, kv_cols), bf16),
            pltpu.VMEM((chunks, w_rows, cols), bf16),
            pltpu.VMEM((chunks, w_rows, cols), bf16),
            pltpu.VMEM((places, 2, local, q_cols), bf16),
            pltpu.VMEM((places, local, q_cols), bf16),
            pltpu.VMEM((places + 1, chunks, local, cols), bf16),
            pltpu.VMEM((chunks, local, cols), f32),
            pltpu.VMEM((local, width), bf16),
            dma((4,)),
            dma((3,)),
            dma((2,)),
            dma((chunks,)),
            dma,
            dma((chunks, seq)),
            dma((chunks, seq)),
            dma((2,)),
            dma((2,)),
            dma((places,)),
            dma((places,)),
            dma((places + 1, chunks)),
            dma((places + 1, chunks)),
        ],
        compiler_params=pltpu.CompilerParams(
            collective_id=0, has_side_effects=True, vmem_limit_bytes=63 * 1024 * 1024
        ),
        cost_estimate=pl.CostEstimate(
            flops=2 * rows * width * (q_cols + 2 * kv_cols + 2 * w_rows),
            bytes_accessed=2 * (rows * width + width * (q_cols + 2 * kv_cols) + w_rows * width),
            transcendentals=0,
        ),
    )(
        tokens,
        w_query,
        key_weight_matrix,
        value_weight_matrix,
        prior_key_cache,
        prior_value_cache,
        w_out,
        pre_gain[None, :],
        post_gain[None, :],
        query_gain[None, :],
        key_norm_gain[None, :],
        cosine,
        sine,
    )


def solution(mesh):
    sizes = (mesh.shape["seq"], mesh.shape["tp"])
    return jax.shard_map(
        functools.partial(sublayer, sizes),
        mesh=mesh,
        in_specs=(
            P("seq", None),
            P(),
            P(None, "tp"),
            P(None, "tp"),
            P(None, "tp"),
            P(),
            P(),
            P(None, "tp"),
            P(None, "tp"),
            P("tp", None),
            P(),
        ),
        out_specs=P(("seq", "tp"), None),
        check_vma=False,
    )
```

profile of v0, /device:TPU:5, one launch (start us, length us, event | category | flops | bytes accessed | tf_op | source)
XLA Modules:
  0.0 158.7 jit_solution(6952045209222041538)
XLA Ops:
  0.0 1.4 broadcast_in_dim.14.pre_ref
  1.4 1.3 broadcast_in_dim.15.post_ref
  2.7 1.9 %fusion = (f32[1024,64]{1,0:T(8,128)S(1)}, f32[1024,64]{1,0:T(8,128)S(1)}, f32[1024,64]{1,0:T(8,128)S(1)}) fusion(f32[64]{0:T(128)S(1)} %multiply_power_fusion, f32[1024]{0:T(1024)S(1)} %add_convert_fusion), kind=kLoop, calls=%fused_computation.4 | loop fusion | flops 131072 | bytes 790784 | tf_op jit(solution)/shard_map/neg | solution.py:492
  4.6 1.3 pad_maximum_fusion
  5.9 150.2 %shard_map.109 = bf16[128,5376]{1,0:T(8,128)(2,1)} custom-call(bf16[1024,5376]{1,0:T(8,128)(2,1)} %tokens_ref.1, bf16[5376,512]{1,0:T(8,128)(2,1)} %wq_ref.1, bf16[5376,256]{1,0:T(8,128)(2,1)} %wk_ref.1, bf16[5376,256]{1,0:T(8,128)(2,1)} %wv_ref.1, bf16[1024,256]{1,0:T(8,128)(2,1)} %pk_ref.1, bf16[1024,256]{1,0:T(8,128)(2,1)} %pv_ref.1, ...), custom_call_target="tpu_custom_call" | custom-call | flops 22548578304 | bytes 27525120 | tf_op jit(solution)/shard_map/pallas_call | solution.py:497
  156.2 2.5 %copy.13 = bf16[128,5376]{1,0:T(8,128)(2,1)} copy(bf16[128,5376]{1,0:T(8,128)(2,1)} %shard_map.109) | data formatting | bytes 2752512
  (2 shorter events, 0.0 us)
where the time goes:
time: 159 us
  Pallas kernels  150 us (94%)
  local copies, waits for them, and re-layouts  5.21 us (3%)
  other arithmetic  3.23 us (2%)
    pallas_call x1, Pallas kernels, sublayer(): pl.pallas_call(functools.partial(kernel, (seq, tp, head, chunks)), out_sh...  150 us

commit v1 on v0

--- a/solution.py
+++ b/solution.py
@@ -2,6 +2,7 @@
 
 import jax
 import jax.numpy as jnp
+import numpy as np
 from jax import lax
 from jax.experimental import pallas as pl
 from jax.experimental.pallas import tpu as pltpu
@@ -15,11 +16,16 @@
 MESH = pl.DeviceIdType.MESH
 
 
-def rotary_tables(half, token_positions):
-    exponent = jnp.arange(half, dtype=jnp.float32) * (-1.0 / half)
-    frequency = jnp.power(jnp.float32(10000.0), exponent)
-    angles = token_positions.astype(jnp.float32)[:, None] * frequency[None, :]
-    return jnp.cos(angles), jnp.sin(angles)
+FINE = 32
+
+
+def rotary_tables(half, first, length):
+    frequency = 10000.0 ** (-np.arange(half, dtype=np.float64) / half)
+    frequency = np.concatenate([frequency, frequency]).astype(np.float32).astype(np.float64)
+    coarse = np.arange(first, first + length, FINE)[:, None] * frequency
+    fine = np.arange(FINE)[:, None] * frequency
+    tables = [np.cos(coarse), np.sin(coarse), np.cos(fine), np.sin(fine)]
+    return [table.astype(np.float32) for table in tables]
 
 
 def chunk_count(width):
@@ -30,6 +36,12 @@
     return 1
 
 
+def helped_chunks(chunks, places):
+    if places < 4:
+        return []
+    return list(range(1, chunks, 2))
+
+
 def orders(places):
     return [
         sorted(range(places), key=lambda r: (-abs(r - p), r < p)) for p in range(places)
@@ -43,10 +55,11 @@
 def kernel(
     dims,
     tokens_ref, wq_ref, wk_ref, wv_ref, pk_ref, pv_ref, wo_ref,
-    pre_ref, post_ref, qg_ref, kg_ref, cos_ref, sin_ref,
+    cc_ref, cs_ref, pre_ref, post_ref, qg_ref, kg_ref, fc_ref, fs_ref,
     out_ref,
-    x_buf, wq_buf, wk_buf, wv_buf, q_buf, k_buf, v_buf, wo_buf, wx_buf, att_buf, got_buf, slots, acc_buf, own_buf,
-    tok_sem, w_sem, prior_sem, wo_sem, own_sem, w_send, w_recv, kv_send, kv_recv, sw_send, sw_recv, s_send, s_recv,
+    x_buf, wq_buf, wk_buf, wv_buf, q_buf, k_buf, v_buf, wo_buf, wx_buf, att_buf, got_buf, slots, acc_buf, own_buf, we_buf, ea_buf, cc_buf, cs_buf, cos_ref, sin_ref,
+    rot_sem, tok_sem, w_sem, prior_sem, wo_sem, own_sem, w_send, w_recv, kv_send, kv_recv, sw_send, sw_recv, s_send, s_recv,
+    e_send, e_recv, ea_send, ea_recv,
 ):
     seq, tp, head, chunks = dims
     rows, width = tokens_ref.shape
@@ -56,6 +69,7 @@
     w_rows = wo_ref.shape[0]
     piece = w_rows // seq
     cols = width // chunks
+    helped = helped_chunks(chunks, places)
     bits = []
     bit = seq // 2
     while bit >= 1:
@@ -67,6 +81,9 @@
     side = t % 2
     p = t // 2
     mate = t + 1 - 2 * side
+    at_end = (p == 0) | (p == places - 1)
+    by_end = (p == 1) | (p == places - 2)
+    end = jnp.where(p == 1, 0, places - 1)
     scale = float(MODEL_WIDTH // HQ) ** (-0.5)
     f32 = jnp.float32
 
@@ -90,7 +107,13 @@
     own_load = pltpu.make_async_copy(tokens_ref.at[pl.ds(pl.multiple_of(t * local, local), local)], own_buf, own_sem)
     for i in range(parts):
         token_load(i).start()
-    for load in weight_loads:
+    weight_loads[0].start()
+    coarse_rows = rows // FINE
+    table_loads = [
+        pltpu.make_async_copy(src.at[pl.ds(pl.multiple_of(s * coarse_rows, 8), coarse_rows)], dst, rot_sem.at[i])
+        for i, (src, dst) in enumerate(((cc_ref, cc_buf), (cs_ref, cs_buf)))
+    ]
+    for load in table_loads:
         load.start()
 
     @pl.when(s == 0)
@@ -174,22 +197,6 @@
         for m in masks(stage):
             w_next(c, stage, m).start()
 
-    def pumps(position):
-        for stage in range(1, stages + 1):
-            lag = -1 if stage == 1 else stage - 1
-            if isinstance(position, int):
-                if position == 0 and stage == 1:
-                    pump(1, 0)
-                c = position - lag
-                if 0 <= c < chunks:
-                    pump(stage, c)
-            else:
-                c = position - lag
-
-                @pl.when((c >= 0) & (c < chunks))
-                def _(stage=stage, c=c):
-                    pump(stage, c)
-
     def w_ready(c):
         if stages == 0:
             w_arrived(c, 0)
@@ -199,17 +206,91 @@
                 w_arrived(c, m + b)
         wo_load(c).wait()
 
+    def e_copy(f, half, m, src, index, device):
+        return pltpu.make_async_remote_copy(
+            src_ref=src,
+            dst_ref=we_buf.at[f, half, pl.ds(pl.multiple_of(index * piece, piece), piece)],
+            send_sem=e_send.at[f, half, m],
+            recv_sem=e_recv.at[f, half, m],
+            device_id=device,
+            device_id_type=MESH,
+        )
+
+    def e_piece(f, half, index):
+        return we_buf.at[f, half, pl.ds(pl.multiple_of(index * piece, piece), piece)]
+
+    def e_first(f, m):
+        index = from_mask(m)
+        src = wo_ref.at[pl.ds(pl.multiple_of(index * piece, piece), piece), pl.ds(helped[f] * cols, cols)]
+        return e_copy(f, 0, m, src, index, (s, 2 * jnp.where(p == 0, 1, places - 2) + side))
+
+    def e_mate(f):
+        return e_copy(f, 1, 0, e_piece(f, 0, s), s, (s, mate))
+
+    def e_next(f, half, stage, m):
+        b = bits[stage - 1]
+        index = from_mask(m)
+        return e_copy(f, half, m + b, e_piece(f, half, index), index, (flipped(s, b), t))
+
+    def e_arrived(f, half, m):
+        index = from_mask(m)
+        e_copy(f, half, m, e_piece(f, half, index), index, (s, mate)).wait_recv()
+
+    def e_pump(stage, f):
+        @pl.when(by_end)
+        def _():
+            if stage == 0:
+                e_arrived(f, 0, 0)
+                e_mate(f).start()
+                return
+            if stage == 1:
+                e_arrived(f, 1, 0)
+            else:
+                for m in masks(stage - 1):
+                    e_arrived(f, 1, m + bits[stage - 2])
+            for m in masks(stage):
+                e_next(f, 1, stage, m).start()
+                if stage == stages:
+                    if m:
+                        e_arrived(f, 0, m)
+                    e_next(f, 0, stage, m).start()
+
+    def e_ready(f):
+        @pl.when(by_end)
+        def _():
+            if stages == 0:
+                e_arrived(f, 1, 0)
+            else:
+                for half in range(2):
+                    for m in masks(stages):
+                        e_arrived(f, half, m + bits[-1])
+
     for c in range(chunks):
         w_first(c).start()
-    for c in range(chunks):
-        wo_load(c).start()
-    own_load.start()
+
+    @pl.when(at_end)
+    def _():
+        for f in range(len(helped)):
+            for m in masks(stages):
+                e_first(f, m).start()
+
+    for load in table_loads:
+        load.wait()
+    sign = jnp.where(lax.broadcasted_iota(jnp.int32, (FINE, head), 1) < head // 2, -1.0, 1.0)
+    for i in range(coarse_rows):
+        far_c, far_s = cc_buf[i : i + 1, :], cs_buf[i : i + 1, :]
+        near_c, near_s = fc_ref[...], fs_ref[...]
+        cos_ref[i * FINE : (i + 1) * FINE, :] = far_c * near_c - far_s * near_s
+        sin_ref[i * FINE : (i + 1) * FINE, :] = (far_s * near_c + far_c * near_s) * sign
 
     group = 32
     tiles = width // LANES
 
     for i in range(parts):
         token_load(i).wait()
+        if i == parts - 1:
+            weight_loads[1].start()
+            weight_loads[2].start()
 
         @pl.loop(0, part // group)
         def _(g, i=i):
@@ -221,10 +302,10 @@
             factor = lax.rsqrt(jnp.sum(sums, axis=-1, keepdims=True) * (1.0 / width) + EPSILON)
             for j in range(tiles):
                 v = x_buf[at, j * LANES : (j + 1) * LANES].astype(f32)
-                gain = pre_ref[:, j * LANES : (j + 1) * LANES]
+                gain = pre_ref[pl.ds(j * LANES, LANES)][None, :]
                 x_buf[at, j * LANES : (j + 1) * LANES] = (v * factor * gain).astype(jnp.bfloat16)
 
-    pumps(0)
+    pump(1, 0)
 
     row_tile = min(512, rows)
 
@@ -242,7 +323,7 @@
             for h in range(size // head):
                 u = raw[:, h * head : (h + 1) * head]
                 mean_square = jnp.mean(u * u, axis=-1, keepdims=True)
-                u = u * lax.rsqrt(mean_square + EPSILON) * gain_ref[...]
+                u = u * lax.rsqrt(mean_square + EPSILON) * gain_ref[...][None, :]
                 u = u * cosine + pltpu.roll(u, head // 2, 1) * sine
                 dst[to, first + h * head : first + (h + 1) * head] = u.astype(jnp.bfloat16)
 
@@ -266,7 +347,6 @@
     def _():
         kv_copy(0).start()
 
-    pumps(1)
     weight_loads[1].wait()
     project(wv_buf, 0, kv_cols, v_buf, WINDOW_SPAN, None)
 
@@ -274,14 +354,17 @@
     def _():
         kv_copy(1).start()
 
-    pumps(2)
     weight_loads[2].wait()
+    for c in range(chunks):
+        wo_load(c).start()
+    own_load.start()
     tile = min(256, q_cols)
-    position = 3
     for j in range(q_cols // tile):
         project(wq_buf, j * tile, tile, q_buf, 0, qg_ref)
-        pumps(position)
-        position += 1
+    for c in range(1, min(3, chunks)):
+        pump(1, c)
+    for stage in range(2, stages + 1):
+        pump(stage, 0)
 
     @pl.when(s == 0)
     def _():
@@ -353,88 +436,187 @@
             device_id_type=MESH,
         )
 
+    def send_on(r, c):
+        @pl.when(r > p)
+        def _():
+            sum_copy(r, r, c, p + 1).start()
+
+        @pl.when(r < p)
+        def _():
+            sum_copy(r, jnp.where(r == p - 1, places, r), c, p - 1).start()
+
+    def add_on(k, r, c):
+        inner = jnp.where(r > p, p, places - 1 - p) > 0
+        total = product(k, c)
+
+        @pl.when(inner)
+        def _():
+            sum_copy(r, r, c, p).wait_recv()
+
+        total = total + jnp.where(inner, slots[r, c].astype(f32), 0.0)
+        slots[r, c] = total.astype(jnp.bfloat16)
+
     def push(k, c):
         r = row_block(k)
-        right = r > p
-        inner = jnp.where(right, p, places - 1 - p) > 0
-        total = product(k, c)
-
-        @pl.when(inner)
-        def _():
-            sum_copy(r, r, c, p).wait_recv()
-
-        total = total + jnp.where(inner, slots[r, c].astype(f32), 0.0)
-        slots[r, c] = total.astype(jnp.bfloat16)
-
-        @pl.when(right)
-        def _():
-            sum_copy(r, r, c, p + 1).start()
-
-        @pl.when(jnp.logical_not(right))
-        def _():
-            sum_copy(r, jnp.where(r == p - 1, places, r), c, p - 1).start()
-
-    early = min(3, chunks)
-    base = position
+        add_on(k, r, c)
+        send_on(r, c)
+
+    def end_product(r, f):
+        return jnp.dot(ea_buf[r, 0], we_buf[f, 0], preferred_element_type=f32) + jnp.dot(
+            ea_buf[r, 1], we_buf[f, 1], preferred_element_type=f32
+        )
+
+    def push_helped(k, c, f):
+        r = row_block(k)
+        help_here = by_end & (r != end)
+
+        @pl.when(help_here)
+        def _():
+            slots[r, c] = (product(k, c) + end_product(r, f)).astype(jnp.bfloat16)
+
+        @pl.when(jnp.logical_not(help_here | at_end))
+        def _():
+            add_on(k, r, c)
+
+        @pl.when(jnp.logical_not(at_end))
+        def _():
+            send_on(r, c)
+
+    def end_rows(k, half, r):
+        src = got_buf.at[k] if half else att_buf.at[k, side]
+        return pltpu.make_async_remote_copy(
+            src_ref=src,
+            dst_ref=ea_buf.at[r, half],
+            send_sem=ea_send.at[k, half],
+            recv_sem=ea_recv.at[r, half],
+            device_id=(s, 2 * jnp.where(p == 0, 1, places - 2) + side),
+            device_id_type=MESH,
+        )
 
     @pl.loop(0, places)
     def _(k):
         attend(k)
         swap(k).start()
-        pumps(base + k)
-
-        @pl.when(k == 1)
-        def _():
-            for c in range(early):
-                w_ready(c)
+
+        @pl.when(k == 0)
+        def _():
+            w_ready(0)
+
+        @pl.when((k < 2) & (k + 3 < chunks))
+        def _():
+            pump(1, k + 3)
+
+        for f in range(min(len(helped), places)):
+            @pl.when(k == f)
+            def _(f=f):
+                e_pump(0, f)
+
+        for f in range(min(len(helped), places - 2)):
+            @pl.when(k == f + 2)
+            def _(f=f):
+                e_pump(1, f)
 
         @pl.when(k >= 1)
         def _():
             swap(k - 1).wait_recv()
-
-            @pl.loop(0, early)
-            def _(c):
-                push(k - 1, c)
-
-    for extra in range(base + places, chunks + stages):
-        pumps(extra)
-
-    @pl.loop(early, chunks)
-    def _(c):
+            push(k - 1, 0)
+
+            if helped:
+                @pl.when(at_end & (k < places - 1))
+                def _():
+                    for half in range(2):
+                        end_rows(k - 1, half, row_block(k - 1)).start()
+
+    for f in range(places, len(helped)):
+        e_pump(0, f)
+    waiting = []
+    for c in range(3, chunks):
+        if c >= 5:
+            waiting.append((c, False))
+        if c in helped and helped.index(c) >= places - 2:
+            waiting.append((c, True))
+    for c in range(1, chunks):
+        taken = 0
+        while waiting and (taken < 2 or waiting[0][0] <= c):
+            which, ends = waiting.pop(0)
+            if stages == 0:
+                continue
+            if ends:
+                e_pump(1, helped.index(which))
+            else:
+                pump(1, which)
+            taken += 1
+        for stage in range(2, stages + 1):
+            pump(stage, c)
+            if c in helped:
+                e_pump(stage, helped.index(c))
         w_ready(c)
-
-        @pl.loop(0, places - 1)
-        def _(k):
-            push(k, c)
-
-    if places == 1:
-        for c in range(early):
-            w_ready(c)
+        if c not in helped:
+            @pl.loop(0, places - 1)
+            def _(k, c=c):
+                push(k, c)
+        else:
+            f = helped.index(c)
+            e_ready(f)
+            if f == 0:
+                @pl.when(by_end)
+                def _():
+                    @pl.loop(0, places)
+                    def _(r):
+                        @pl.when((r != end) & (r != p))
+                        def _():
+                            for half in range(2):
+                                end_rows(0, half, r).wait_recv()
+
+            @pl.loop(0, places - 1)
+            def _(k, c=c, f=f):
+                push_helped(k, c, f)
+    if helped:
+        @pl.when(at_end)
+        def _():
+            for half in range(2):
+                end_rows(places - 2, half, row_block(places - 2)).start()
+
     last = places - 1
     swap(last).wait_recv()
     own_load.wait()
 
     def finish(c, square):
         total = product(last, c)
-
-        @pl.when(p > 0)
+        ahead, behind = p > 0, p < places - 1
+        if c in helped:
+            ahead, behind = ahead & (p != 1), behind & (p != places - 2)
+            acc_buf[c] = total
+
+            @pl.when(by_end)
+            def _():
+                if c == helped[0]:
+                    for half in range(2):
+                        end_rows(0, half, p).wait_recv()
+                acc_buf[c] += end_product(p, helped.index(c))
+
+            total = acc_buf[c]
+
+        @pl.when(ahead)
         def _():
             sum_copy(p, p, c, p).wait_recv()
 
-        @pl.when(p < places - 1)
+        @pl.when(behind)
         def _():
             sum_copy(p, places, c, p).wait_recv()
 
-        total = total + jnp.where(p > 0, slots[p, c].astype(f32), 0.0)
-        total = total + jnp.where(p < places - 1, slots[places, c].astype(f32), 0.0)
+        total = total + jnp.where(ahead, slots[p, c].astype(f32), 0.0)
+        total = total + jnp.where(behind, slots[places, c].astype(f32), 0.0)
         acc_buf[c] = total
         return square + jnp.sum(total * total, axis=-1, keepdims=True)
 
-    square = lax.fori_loop(0, chunks, finish, jnp.zeros((local, 1), f32))
+    square = jnp.zeros((local, 1), f32)
+    for c in range(chunks):
+        square = finish(c, square)
     factor = lax.rsqrt(square * (1.0 / width) + EPSILON)
     for c in range(chunks):
         at = slice(c * cols, (c + 1) * cols)
-        out_ref[:, at] = (own_buf[:, at].astype(f32) + acc_buf[c] * factor * post_ref[:, at]).astype(out_ref.dtype)
+        out_ref[:, at] = (own_buf[:, at].astype(f32) + acc_buf[c] * factor * post_ref[pl.ds(c * cols, cols)][None, :]).astype(out_ref.dtype)
 
     for c in range(chunks):
         w_first(c).wait_send()
@@ -458,9 +640,35 @@
         def _():
             r = row_block(k)
 
-            @pl.loop(0, chunks)
-            def _(c):
-                sum_copy(r, r, c, p).wait_send()
+            for c in range(chunks):
+                if c in helped:
+                    @pl.when(jnp.logical_not(at_end))
+                    def _(c=c):
+                        sum_copy(r, r, c, p).wait_send()
+                else:
+                    sum_copy(r, r, c, p).wait_send()
+
+    if helped:
+        @pl.when(at_end)
+        def _():
+            for f in range(len(helped)):
+                for m in masks(stages):
+                    e_first(f, m).wait_send()
+
+            @pl.loop(0, places - 1)
+            def _(k):
+                for half in range(2):
+                    end_rows(k, half, row_block(k)).wait_send()
+
+        @pl.when(by_end)
+        def _():
+            for f in range(len(helped)):
+                e_mate(f).wait_send()
+                for stage in range(1, stages + 1):
+                    for m in masks(stage):
+                        e_next(f, 1, stage, m).wait_send()
+                        if stage == stages:
+                            e_next(f, 0, stage, m).wait_send()
 
 
 def sublayer(
@@ -486,10 +694,8 @@
     places = tp // 2
     chunks = chunk_count(width)
     cols = width // chunks
-    token_positions = WINDOW_SPAN + lax.axis_index("seq") * rows + jnp.arange(rows, dtype=jnp.int32)
-    cosine, sine = rotary_tables(head // 2, token_positions)
-    cosine = jnp.concatenate([cosine, cosine], axis=1)
-    sine = jnp.concatenate([-sine, sine], axis=1)
+    helped = len(helped_chunks(chunks, places))
+    tables = rotary_tables(head // 2, WINDOW_SPAN, seq * rows)
     bf16, f32 = jnp.bfloat16, jnp.float32
     dma = pltpu.SemaphoreType.DMA
     anywhere = pl.BlockSpec(memory_space=pl.ANY)
@@ -497,7 +703,7 @@
     return pl.pallas_call(
         functools.partial(kernel, (seq, tp, head, chunks)),
         out_shape=jax.ShapeDtypeStruct((local, width), tokens.dtype),
-        in_specs=[anywhere] * 7 + [vmem] * 6,
+        in_specs=[anywhere] * 9 + [vmem] * 6,
         out_specs=vmem,
         scratch_shapes=[
             pltpu.VMEM((rows, width), bf16),
@@ -514,6 +720,13 @@
             pltpu.VMEM((places + 1, chunks, local, cols), bf16),
             pltpu.VMEM((chunks, local, cols), f32),
             pltpu.VMEM((local, width), bf16),
+            pltpu.VMEM((max(helped, 1), 2, w_rows, cols), bf16),
+            pltpu.VMEM((places, 2, local, q_cols), bf16),
+            pltpu.VMEM((rows // FINE, head), f32),
+            pltpu.VMEM((rows // FINE, head), f32),
+            pltpu.VMEM((rows, head), f32),
+            pltpu.VMEM((rows, head), f32),
+            dma((2,)),
             dma((4,)),
             dma((3,)),
             dma((2,)),
@@ -527,6 +740,10 @@
             dma((places,)),
             dma((places + 1, chunks)),
             dma((places + 1, chunks)),
+            dma((max(helped, 1), 2, seq)),
+            dma((max(helped, 1), 2, seq)),
+            dma((places, 2)),
+            dma((places, 2)),
         ],
         compiler_params=pltpu.CompilerParams(
             collective_id=0, has_side_effects=True, vmem_limit_bytes=63 * 1024 * 1024
@@ -544,12 +761,14 @@
         prior_key_cache,
         prior_value_cache,
         w_out,
-        pre_gain[None, :],
-        post_gain[None, :],
-        query_gain[None, :],
-        key_norm_gain[None, :],
-        cosine,
-        sine,
+        tables[0],
+        tables[1],
+        pre_gain,
+        post_gain,
+        query_gain,
+        key_norm_gain,
+        tables[2],
+        tables[3],
     )
 
 

time: 159 us -> 131 us (0.82)
  the two profiles are of different devices: /device:TPU:5 before, /device:TPU:0 now
where the time goes in v1:
time: 131 us
  Pallas kernels  129 us (98%)
  local copies, waits for them, and re-layouts  2.51 us (2%)
    pallas_call x1, Pallas kernels, sublayer(): pl.pallas_call(functools.partial(kernel, (seq, tp, head, chunks)), out_sh...  129 us

profile of v1, /device:TPU:0, one launch (start us, length us, event | category | flops | bytes accessed | tf_op | source)
XLA Modules:
  0.0 131.1 jit_solution(11284132528084740598)
XLA Ops:
  0.0 128.6 %shard_map.145 = bf16[128,5376]{1,0:T(8,128)(2,1)} custom-call(bf16[1024,5376]{1,0:T(8,128)(2,1)} %tokens_ref.1, bf16[5376,512]{1,0:T(8,128)(2,1)} %wq_ref.1, bf16[5376,256]{1,0:T(8,128)(2,1)} %wk_ref.1, bf16[5376,256]{1,0:T(8,128)(2,1)} %wv_ref.1, bf16[1024,256]{1,0:T(8,128)(2,1)} %pk_ref.1, bf16[1024,256]{1,0:T(8,128)(2,1)} %pv_ref.1, ...), custom_call_target="tpu_custom_call" | custom-call | flops 22548578304 | bytes 27525120 | tf_op jit(solution)/shard_map/pallas_call | solution.py:703
  128.6 2.5 %copy.17 = bf16[128,5376]{1,0:T(8,128)(2,1)} copy(bf16[128,5376]{1,0:T(8,128)(2,1)} %shard_map.145) | data formatting | bytes 2752512

commit v2 on v1

--- a/solution.py
+++ b/solution.py
@@ -13,6 +13,7 @@
 WINDOW_SPAN = 1024
 EPSILON = 1e-06
 LANES = 128
+LOG2E = 1.4426950408889634
 MESH = pl.DeviceIdType.MESH
 
 
@@ -43,9 +44,11 @@
 
 
 def orders(places):
-    return [
-        sorted(range(places), key=lambda r: (-abs(r - p), r < p)) for p in range(places)
-    ]
+    table = []
+    for p in range(places):
+        above, below = list(range(places - 1, p, -1)), list(range(p))
+        table.append((above + below if len(above) >= len(below) else below + above) + [p])
+    return table
 
 
 def flipped(index, bit):
@@ -265,7 +268,8 @@
                     for m in masks(stages):
                         e_arrived(f, half, m + bits[-1])
 
-    for c in range(chunks):
+    prompt = chunks
+    for c in range(prompt):
         w_first(c).start()
 
     @pl.when(at_end)
@@ -391,9 +395,9 @@
     def attend(k):
         r = row_block(k)
         first = pl.multiple_of(r * count, count)
-        row_ids = lax.broadcasted_iota(jnp.int32, (count, span), 0)
-        col_ids = lax.broadcasted_iota(jnp.int32, (count, span), 1)
-        allowed = (col_ids > row_ids) & (col_ids <= row_ids + WINDOW_SPAN)
+        row_ids = lax.broadcasted_iota(jnp.int32, (count, count), 0)
+        col_ids = lax.broadcasted_iota(jnp.int32, (count, count), 1)
+        after = col_ids > row_ids
         for kv in range(kv_cols // head):
             keys = k_buf[pl.ds(first, span), kv * head : (kv + 1) * head]
             values = v_buf[pl.ds(first, span), kv * head : (kv + 1) * head]
@@ -402,9 +406,16 @@
                 scores = lax.dot_general(
                     q_buf[pl.ds(first, count), at], keys, (((1,), (1,)), ((), ())), preferred_element_type=f32
                 )
-                scores = jnp.where(allowed, scores * scale, -jnp.inf)
+                scores = jnp.concatenate(
+                    [
+                        jnp.where(after, scores[:, :count], -jnp.inf),
+                        scores[:, count:WINDOW_SPAN],
+                        jnp.where(after, -jnp.inf, scores[:, WINDOW_SPAN:]),
+                    ],
+                    axis=1,
+                )
                 highest = jnp.max(scores, axis=-1, keepdims=True)
-                weights = jnp.exp(scores - highest)
+                weights = jnp.exp2((scores - highest) * (scale * LOG2E))
                 total = jnp.sum(weights, axis=-1, keepdims=True)
                 mixed = jnp.dot(weights.astype(jnp.bfloat16), values, preferred_element_type=f32)
                 mixed = (mixed / total).astype(jnp.bfloat16)
@@ -472,6 +483,9 @@
 
         @pl.when(help_here)
         def _():
+            if f == 0:
+                for half in range(2):
+                    end_rows(0, half, r).wait_recv()
             slots[r, c] = (product(k, c) + end_product(r, f)).astype(jnp.bfloat16)
 
         @pl.when(jnp.logical_not(help_here | at_end))
@@ -502,9 +516,15 @@
         def _():
             w_ready(0)
 
-        @pl.when((k < 2) & (k + 3 < chunks))
-        def _():
-            pump(1, k + 3)
+        for c in range(prompt, min(chunks, prompt + places)):
+            @pl.when(k == c - prompt)
+            def _(c=c):
+                w_first(c).start()
+
+        if chunks > 3:
+            @pl.when(k == 0)
+            def _():
+                pump(1, 3)
 
         for f in range(min(len(helped), places)):
             @pl.when(k == f)
@@ -522,16 +542,19 @@
             push(k - 1, 0)
 
             if helped:
-                @pl.when(at_end & (k < places - 1))
+                @pl.when(at_end & (k == places - 2))
                 def _():
-                    for half in range(2):
-                        end_rows(k - 1, half, row_block(k - 1)).start()
-
+                    for kk in range(places - 2):
+                        for half in range(2):
+                            end_rows(kk, half, row_block(kk)).start()
+
+    for c in range(prompt + places, chunks):
+        w_first(c).start()
     for f in range(places, len(helped)):
         e_pump(0, f)
     waiting = []
     for c in range(3, chunks):
-        if c >= 5:
+        if c >= 4:
             waiting.append((c, False))
         if c in helped and helped.index(c) >= places - 2:
             waiting.append((c, True))
@@ -558,16 +581,6 @@
         else:
             f = helped.index(c)
             e_ready(f)
-            if f == 0:
-                @pl.when(by_end)
-                def _():
-                    @pl.loop(0, places)
-                    def _(r):
-                        @pl.when((r != end) & (r != p))
-                        def _():
-                            for half in range(2):
-                                end_rows(0, half, r).wait_recv()
-
             @pl.loop(0, places - 1)
             def _(k, c=c, f=f):
                 push_helped(k, c, f)

time: 131 us -> 125 us (0.954)
  Pallas kernels: 129 us -> 122 us
    pallas_call x1, Pallas kernels: 129 us -> 122 us  [sublayer(): pl.pallas_call(functools.partial(kernel, (seq, tp, head, chunks)), out_sh...]
where the time goes in v2:
time: 125 us; the launch traced here: 124 us
  Pallas kernels  122 us (98%)
  local copies, waits for them, and re-layouts  2.51 us (2%)
    pallas_call x1, Pallas kernels, sublayer(): pl.pallas_call(functools.partial(kernel, (seq, tp, head, chunks)), out_sh...  122 us
    unnamed x1, local copies, waits for them, and re-layouts  2.51 us

profile of v2, /device:TPU:0, one launch (start us, length us, event | category | flops | bytes accessed | tf_op | source)
XLA Modules:
  0.0 124.3 jit_solution(1287188485900222677)
XLA Ops:
  0.0 121.8 %shard_map.145 = bf16[128,5376]{1,0:T(8,128)(2,1)} custom-call(bf16[1024,5376]{1,0:T(8,128)(2,1)} %tokens_ref.1, bf16[5376,512]{1,0:T(8,128)(2,1)} %wq_ref.1, bf16[5376,256]{1,0:T(8,128)(2,1)} %wk_ref.1, bf16[5376,256]{1,0:T(8,128)(2,1)} %wv_ref.1, bf16[1024,256]{1,0:T(8,128)(2,1)} %pk_ref.1, bf16[1024,256]{1,0:T(8,128)(2,1)} %pv_ref.1, ...), custom_call_target="tpu_custom_call" | custom-call | flops 22548578304 | bytes 27525120 | tf_op jit(solution)/shard_map/pallas_call | solution.py:716
  121.8 2.5 %copy.17 = bf16[128,5376]{1,0:T(8,128)(2,1)} copy(bf16[128,5376]{1,0:T(8,128)(2,1)} %shard_map.145) | data formatting | bytes 2752512
